TPU v7x, 32 devices: a whole 2x2x4 slice. The times are simulated.
32 devices in a mesh: face: 2 (over y), fy: 4 (over x, core), fx: 4 (over z).
Axes of the slice: x: 2, y: 2, z: 4, core: 2. Of those that a mesh axis runs over, the one named last changes fastest.
Arguments:
- state: float32 [6, 32, 32, 192], P('face', 'fy', 'fx'), may hold values from -6 to 6
- jacobian: float32 [6, 32, 32], P('face', 'fy', 'fx'), may hold values from 0.5 to 2
- metric_diag: float32 [2, 6, 32, 32], P(None, 'face', 'fy', 'fx'), may hold values from 0.6 to 1.4
- metric_cross: float32 [6, 32, 32], P('face', 'fy', 'fx'), may hold values from -0.3 to 0.3
- coriolis: float32 [6, 32, 32], P('face', 'fy', 'fx'), may hold values from -2 to 2
- nbr_face: int32 [6, 4], replicated, may hold values from 0 to 5, as said below
- nbr_edge: int32 [6, 4], replicated, may hold values from 0 to 3, as said below
Outputs:
- updated: float32 [6, 32, 32, 192], P('face', 'fy', 'fx')
Inputs may be any that keep to these rules, and one draw needn't show every extreme that they name: Edge e of a face is 0 south (row 0), 1 east (last column), 2 north (last row), 3 west (column 0). Edge e of face f is glued to edge nbr_edge[f, e] of face nbr_face[f, e], and that edge back to it; the 6 faces are glued as the surface of a cube, three faces at each corner, the two glued edges running in opposite senses when both are read counterclockwise. `nbr_edge`: see nbr_face.
All inputs are finite; a program needn't handle non-finite values.
Results may differ from a plain program's by a relative error of at most 0.0001.
Values sent between devices are 32-bit elements; how exact they have to be, the bound alone decides.
A program may use at most 64 MiB of HBM per device.

v0:
```python
import jax
import jax.numpy as jnp
import numpy as np
from jax import lax
from jax.sharding import PartitionSpec as P

time_step = 0.05
hyper_coeff = 0.0005


def padded(cells, sides, width):
    for axis, dim in sides:
        count = lax.axis_size(axis)
        ends = count - 1
        head = lax.slice_in_dim(cells, 0, width, axis=dim)
        tail = lax.slice_in_dim(cells, cells.shape[dim] - width, cells.shape[dim], axis=dim)
        cells = jnp.concatenate(
            [
                lax.ppermute(tail, axis, [(i, (i + 1) % count) for i in range(ends)]),
                cells,
                lax.ppermute(head, axis, [((i + 1) % count, i) for i in range(ends)]),
            ],
            axis=dim,
        )
    return cells


def deriv_table():
    gll_nodes = np.array([-1.0, -1.0 / np.sqrt(5.0), 1.0 / np.sqrt(5.0), 1.0])
    bary_weights = np.ones(4)
    for j in range(4):
        for m in range(4):
            if m != j:
                bary_weights[j] = bary_weights[j] / (gll_nodes[j] - gll_nodes[m])
    matrix = np.zeros((4, 4))
    for i in range(4):
        for j in range(4):
            if i != j:
                matrix[i, j] = bary_weights[j] / bary_weights[i] / (gll_nodes[i] - gll_nodes[j])
        matrix[i, i] = -np.sum(matrix[i])
    return matrix


def along_x(values):
    face_count, row_count, col_count, chan_count = values.shape
    blocks = values.reshape(face_count, row_count, col_count // 4, 4, chan_count)
    result = jnp.einsum(
        "jk,abekc->abejc",
        jnp.asarray(deriv_table(), jnp.float32),
        blocks,
        precision=lax.Precision.HIGHEST,
    )
    return result.reshape(values.shape)


def along_y(values):
    face_count, row_count, col_count, chan_count = values.shape
    blocks = values.reshape(face_count, row_count // 4, 4, col_count, chan_count)
    result = jnp.einsum(
        "ik,aekxc->aeixc",
        jnp.asarray(deriv_table(), jnp.float32),
        blocks,
        precision=lax.Precision.HIGHEST,
    )
    return result.reshape(values.shape)


def mass_of(jacobian):
    weights = jnp.asarray([1.0 / 6.0, 5.0 / 6.0, 5.0 / 6.0, 1.0 / 6.0], jnp.float32)
    row_weight = jnp.tile(weights, jacobian.shape[1] // 4)
    col_weight = jnp.tile(weights, jacobian.shape[2] // 4)
    return jacobian * row_weight[None, :, None] * col_weight[None, None, :]


def tendency(state, geometry, planet):
    volume, metric_xx, metric_yy, metric_xy = geometry
    levels = state.shape[-1] // 3
    wind_u = state[..., :levels]
    wind_v = state[..., levels : 2 * levels]
    temper = state[..., 2 * levels :]
    contra_u = metric_xx * wind_u + metric_xy * wind_v
    contra_v = metric_xy * wind_u + metric_yy * wind_v
    energy = 0.5 * (wind_u * contra_u + wind_v * contra_v) + temper
    xderivs = along_x(jnp.concatenate([wind_v, temper, energy], -1))
    yderivs = along_y(jnp.concatenate([wind_u, temper, energy], -1))
    absolute = (xderivs[..., :levels] - yderivs[..., :levels]) / volume + planet
    tend_u = absolute * volume * contra_v - xderivs[..., 2 * levels :]
    tend_v = -absolute * volume * contra_u - yderivs[..., 2 * levels :]
    tend_t = -(
        contra_u * xderivs[..., levels : 2 * levels] + contra_v * yderivs[..., levels : 2 * levels]
    )
    return state + time_step * jnp.concatenate([tend_u, tend_v, tend_t], -1)


def laplace(values, geometry):
    volume, metric_xx, metric_yy, metric_xy = geometry
    grad_x = along_x(values)
    grad_y = along_y(values)
    flux_x = volume * (metric_xx * grad_x + metric_xy * grad_y)
    flux_y = volume * (metric_xy * grad_x + metric_yy * grad_y)
    return (along_x(flux_x) + along_y(flux_y)) / volume


def combine(values, axis):
    length = values.shape[axis] - 2
    positions = jnp.arange(length)
    leading = (positions % 4 == 0).astype(jnp.float32)
    trailing = (positions % 4 == 3).astype(jnp.float32)
    broad_shape = [1, 1, 1, 1]
    broad_shape[axis] = length
    leading = leading.reshape(broad_shape)
    trailing = trailing.reshape(broad_shape)
    middle = lax.slice_in_dim(values, 1, length + 1, axis=axis)
    previous = lax.slice_in_dim(values, 0, length, axis=axis)
    following = lax.slice_in_dim(values, 2, length + 2, axis=axis)
    return middle + leading * previous + trailing * following


def rotate(segment, quarter, levels):
    cosine = ((quarter == 0).astype(jnp.float32) - (quarter == 2).astype(jnp.float32))[..., None]
    sine_part = ((quarter == 1).astype(jnp.float32) - (quarter == 3).astype(jnp.float32))[..., None]
    wind_u = segment[..., :levels]
    wind_v = segment[..., levels : 2 * levels]
    return jnp.concatenate(
        [
            cosine * wind_u - sine_part * wind_v,
            sine_part * wind_u + cosine * wind_v,
            segment[..., 2 * levels :],
        ],
        -1,
    )


def in_face(values):
    across = combine(padded(values, (("fx", 2),), 1), 2)
    return combine(padded(across, (("fy", 1),), 1), 1)


def place_pieces(
    got_flat,
    got_tall,
    vector,
    nbr_edge,
    flat_edge,
    tall_edge,
    on_south,
    on_west,
    flat_start,
    tall_start,
    face_local,
    side_nodes,
    chan_count,
    levels,
):
    edge_ids = jnp.arange(4, dtype=jnp.int32)
    flat_target = nbr_edge[:, flat_edge]
    tall_target = nbr_edge[:, tall_edge]
    if vector:
        got_flat = rotate(got_flat, ((flat_target - flat_edge + 2) % 4)[None, :, None], levels)
        got_tall = rotate(got_tall, ((tall_target - tall_edge + 2) % 4)[None, :, None], levels)
    got_flat = jnp.where(on_south, got_flat[:, :, ::-1], got_flat)
    got_tall = jnp.where(on_west, got_tall, got_tall[:, :, ::-1])
    flat_pick = (flat_target[:, None] == edge_ids[None, :]).astype(jnp.float32)
    tall_pick = (tall_target[:, None] == edge_ids[None, :]).astype(jnp.float32)
    flat_rims = jnp.einsum("se,gsjc->gejc", flat_pick, got_flat, precision=lax.Precision.HIGHEST)
    tall_rims = jnp.einsum("se,gsjc->gejc", tall_pick, got_tall, precision=lax.Precision.HIGHEST)
    empty_rims = jnp.zeros((face_local, 4, side_nodes, chan_count), jnp.float32)
    rim_strips = lax.dynamic_update_slice(empty_rims, flat_rims, (0, 0, flat_start, 0))
    return rim_strips + lax.dynamic_update_slice(empty_rims, tall_rims, (0, 0, tall_start, 0))


def outgoing(
    summed, nbr_face, face_ids, flat_edge, tall_edge, on_south, on_west, flat_live, tall_live
):
    row_count = summed.shape[1]
    col_count = summed.shape[2]
    all_faces = jnp.arange(nbr_face.shape[0], dtype=jnp.int32)
    flat_piece = jnp.where(on_south, summed[:, 0], summed[:, row_count - 1])
    tall_piece = jnp.where(on_west, summed[:, :, 0], summed[:, :, col_count - 1])
    flat_dest = nbr_face[face_ids, flat_edge]
    tall_dest = nbr_face[face_ids, tall_edge]
    flat_send = ((all_faces[:, None] == flat_dest[None, :]) & flat_live).astype(jnp.float32)
    tall_send = ((all_faces[:, None] == tall_dest[None, :]) & tall_live).astype(jnp.float32)
    return (
        flat_send[:, :, None, None] * flat_piece[None],
        tall_send[:, :, None, None] * tall_piece[None],
    )


def assemble(values, vector, nbr_face, nbr_edge):
    summed = in_face(values)
    face_local, row_count, col_count, chan_count = summed.shape
    levels = chan_count // 3
    row_index = lax.axis_index("fy")
    col_index = lax.axis_index("fx")
    side_nodes = row_count * lax.axis_size("fy")
    face_ids = lax.axis_index("face") * face_local + jnp.arange(face_local, dtype=jnp.int32)
    on_south = row_index == 0
    on_north = row_index == lax.axis_size("fy") - 1
    on_west = col_index == 0
    on_east = col_index == lax.axis_size("fx") - 1
    flat_live = on_south | on_north
    tall_live = on_west | on_east
    flat_edge = jnp.where(on_south, 0, 2).astype(jnp.int32)
    tall_edge = jnp.where(on_west, 3, 1).astype(jnp.int32)
    flat_start = jnp.where(
        on_south, side_nodes - (col_index + 1) * col_count, col_index * col_count
    )
    tall_start = jnp.where(on_west, row_index * row_count, side_nodes - (row_index + 1) * row_count)
    send_flat, send_tall = outgoing(
        summed, nbr_face, face_ids, flat_edge, tall_edge, on_south, on_west, flat_live, tall_live
    )
    got_flat, got_tall = (
        lax.all_to_all(send_flat, "face", split_axis=0, concat_axis=1, tiled=True),
        lax.all_to_all(send_tall, "face", split_axis=0, concat_axis=1, tiled=True),
    )
    rim_strips = place_pieces(
        got_flat,
        got_tall,
        vector,
        nbr_edge,
        flat_edge,
        tall_edge,
        on_south,
        on_west,
        flat_start,
        tall_start,
        face_local,
        side_nodes,
        chan_count,
        levels,
    )
    flat_lines = jnp.stack([rim_strips[:, 0], rim_strips[:, 2, ::-1]], axis=1)
    flat_lines = flat_lines.reshape(face_local, 2, lax.axis_size("fx"), col_count, chan_count)
    tall_lines = jnp.stack([rim_strips[:, 1], rim_strips[:, 3, ::-1]], axis=1)
    tall_lines = tall_lines.reshape(face_local, 2, lax.axis_size("fy"), row_count, chan_count)
    flat_whole = lax.psum(flat_lines, "fy")
    tall_whole = lax.psum(tall_lines, "fx")
    flat_block = lax.psum_scatter(flat_whole, "fx", scatter_dimension=2, tiled=True)
    tall_block = lax.psum_scatter(tall_whole, "fy", scatter_dimension=2, tiled=True)
    flat_add = jnp.where(on_south, flat_block[:, 0, 0], flat_block[:, 1, 0])
    tall_add = jnp.where(on_west, tall_block[:, 1, 0], tall_block[:, 0, 0])
    result = summed.at[:, 0].add(jnp.where(on_south, flat_add, 0.0))
    result = result.at[:, row_count - 1].add(jnp.where(on_north, flat_add, 0.0))
    result = result.at[:, :, 0].add(jnp.where(on_west, tall_add, 0.0))
    result = result.at[:, :, col_count - 1].add(jnp.where(on_east, tall_add, 0.0))
    return result


def per_device(state, jacobian, metric_diag, metric_cross, coriolis, nbr_face, nbr_edge):
    node_mass = mass_of(jacobian)[..., None]
    total_mass = assemble(node_mass, False, nbr_face, nbr_edge)
    geometry = (
        jacobian[..., None],
        metric_diag[0][..., None],
        metric_diag[1][..., None],
        metric_cross[..., None],
    )
    raw = tendency(state, geometry, coriolis[..., None])
    sectioned = assemble(node_mass * raw, True, nbr_face, nbr_edge) / total_mass
    first_lap = (
        assemble(node_mass * laplace(sectioned, geometry), True, nbr_face, nbr_edge) / total_mass
    )
    second_lap = (
        assemble(node_mass * laplace(first_lap, geometry), True, nbr_face, nbr_edge) / total_mass
    )
    return sectioned - hyper_coeff * second_lap


def solution(mesh):
    return jax.shard_map(
        per_device,
        mesh=mesh,
        in_specs=(
            P("face", "fy", "fx", None),
            P("face", "fy", "fx"),
            P(None, "face", "fy", "fx"),
            P("face", "fy", "fx"),
            P("face", "fy", "fx"),
            P(),
            P(),
        ),
        out_specs=P("face", "fy", "fx", None),
        check_vma=False,
    )
```

profile of v0, /device:TPU:0, one launch (start us, length us, event | category | flops | bytes accessed | tf_op | source)
XLA Modules:
  0.0 370.9 jit_solution(3466996314126042414)
XLA Ops:
  14.4 5.6 %collective-permute-start = (f32[3,8,1,192]{3,2,0,1:T(1,128)S(1)}, f32[3,8,1,192]{3,2,0,1:T(1,128)S(1)}, u32[]{:S(2)}, u32[]{:S(2)}) collective-permute-start(f32[3,8,1,192]{3,2,0,1:T(1,128)S(1)} %slice.902), channel_id=1, source_target_pairs={{0,1},{1,2},{2,3},{4,5},{5,6},{6,7},{8,9},{9,10},{10,11},{12,13},{... | collective-permute-start | bytes 55304 | tf_op jit(solution)/shard_map/ppermute | solution.py:19
  21.4 4.5 %collective-permute-start.4 = (f32[3,8,1,1]{2,1,0,3:T(8,128)S(1)}, f32[3,8,1,1]{2,1,0,3:T(8,128)S(1)}, u32[]{:S(2)}, u32[]{:S(2)}) collective-permute-start(f32[3,8,1,1]{2,1,0,3:T(8,128)S(1)} %get-tuple-element.262), channel_id=1, source_target_pairs={{0,1},{1,2},{2,3},{4,5},{5,6},{6,7},{8,9},{9,10},{10,11},{12,13},{... | collective-permute-start | bytes 296 | tf_op jit(solution)/shard_map/ppermute | solution.py:19
  37.2 3.2 all-to-all-start.2
  41.1 3.1 all-to-all-done.2
  44.3 3.2 all-to-all-start.3
  47.6 3.7 all-to-all-done.3
  54.1 3.0 collective-permute-start.2
  57.2 13.3 %all-reduce.4 = f32[3,2,4,8,1]{3,1,4,0,2:T(2,128)S(1)} all-reduce(f32[3,2,4,8,1]{3,1,4,0,2:T(2,128)S(1)} %copy.284), channel_id=5, replica_groups=mesh['face'=2,'fy'=4,'fx'=4] {'fy'}, use_global_device_ids=true, to_apply=%region_7.8.clone | all-reduce | flops 192 | bytes 1536
  71.4 3.4 all-to-all-start
  75.7 3.7 %all-to-all-done = f32[6,3,8,192]{3,2,1,0:T(8,128)S(1)} async-done(((f32[6,3,8,192]{3,2,1,0:T(8,128)}), f32[6,3,8,192]{3,2,1,0:T(8,128)S(1)}, u32[]{:S(2)}, u32[]{:S(2)}) %all-to-all-start) | async-done | bytes 110624 | tf_op jit(solution)/shard_map/all_to_all | solution.py:214
  79.4 3.4 all-to-all-start.1
  83.3 4.1 %all-to-all-done.1 = f32[6,3,8,192]{3,2,1,0:T(8,128)S(1)} async-done(((f32[6,3,8,192]{3,2,1,0:T(8,128)}), f32[6,3,8,192]{3,2,1,0:T(8,128)S(1)}, u32[]{:S(2)}, u32[]{:S(2)}) %all-to-all-start.1) | async-done | bytes 110624 | tf_op jit(solution)/shard_map/all_to_all | solution.py:215
  91.5 33.0 %all-reduce.13.cloned.1.call-done = f32[3,2,4,8,192]{4,3,0,2,1:T(8,128)} async-done(((f32[3,2,4,8,192]{4,3,0,2,1:T(8,128)}), f32[3,2,4,8,192]{4,3,0,2,1:T(8,128)}) %all-reduce.13.cloned.1.call-update) | async-done | bytes 147472
  126.8 18.5 %all-reduce.7 = (f32[3,2,1,8,192]{4,1,3,2,0:T(2,128)S(1)}, f32[3,2,4,8,1]{3,1,4,0,2:T(2,128)S(1)}, f32[3,2,1,8,1]{3,1,4,0,2:T(2,128)S(1)}) all-reduce(f32[3,2,1,8,192]{4,1,3,2,0:T(2,128)S(1)} %copy.277, f32[3,2,4,8,1]{3,1,4,0,2:T(2,128)S(1)} %copy.281, ...), channel_id=1, replica_groups=mesh['face'=2,'fy'=4,'fx'=4] {'fx'}, use_global_device_ids=true, to_apply=%region_2.3 | all-reduce | flops 9456 | bytes 75648 | tf_op jit(solution)/shard_map/psum | solution.py:238
  145.9 10.7 %all-reduce.8 = (f32[3,2,1,8,192]{4,3,0,2,1:T(8,128)S(1)}, f32[3,2,1,8,1]{3,1,4,0,2:T(2,128)S(1)}) all-reduce(f32[3,2,1,8,192]{4,3,0,2,1:T(8,128)S(1)} %constant_dynamic-slice_fusion.6, f32[3,2,1,8,1]{3,1,4,0,2:T(2,128)S(1)} %constant_dynamic-slice_fusion.5), channel_id=1, replica_groups=mesh['face'=2,'fy'=4,'fx'=4] {'fy'}, use_global_device_ids=true, to_apply=%region_0.1 | all-reduce | flops 9264 | bytes 74112 | tf_op jit(solution)/shard_map/psum | solution.py:237
  161.9 4.5 %collective-permute-start.8 = (f32[3,8,1,192]{3,2,0,1:T(1,128)S(1)}, f32[3,8,1,192]{3,2,0,1:T(1,128)S(1)}, u32[]{:S(2)}, u32[]{:S(2)}) collective-permute-start(f32[3,8,1,192]{3,2,0,1:T(1,128)S(1)} %get-tuple-element.230), channel_id=1, source_target_pairs={{0,1},{1,2},{2,3},{4,5},{5,6},{6,7},{8,9},{9,10},{10,11},{12,13},{... | collective-permute-start | bytes 55304 | tf_op jit(solution)/shard_map/ppermute | solution.py:19
  169.3 3.2 collective-permute-start.10
  174.1 3.4 all-to-all-start.4
  178.3 4.0 %all-to-all-done.4 = f32[6,3,8,192]{3,2,1,0:T(8,128)S(1)} async-done(((f32[6,3,8,192]{3,2,1,0:T(8,128)}), f32[6,3,8,192]{3,2,1,0:T(8,128)S(1)}, u32[]{:S(2)}, u32[]{:S(2)}) %all-to-all-start.4) | async-done | bytes 110624 | tf_op jit(solution)/shard_map/all_to_all | solution.py:214
  182.3 3.4 all-to-all-start.5
  186.2 4.3 %all-to-all-done.5 = f32[6,3,8,192]{3,2,1,0:T(8,128)S(1)} async-done(((f32[6,3,8,192]{3,2,1,0:T(8,128)}), f32[6,3,8,192]{3,2,1,0:T(8,128)S(1)}, u32[]{:S(2)}, u32[]{:S(2)}) %all-to-all-start.5) | async-done | bytes 110624 | tf_op jit(solution)/shard_map/all_to_all | solution.py:215
  193.8 35.0 %all-reduce.15.cloned.1.call-done = f32[3,2,4,8,192]{4,3,0,2,1:T(8,128)} async-done(((f32[3,2,4,8,192]{4,3,0,2,1:T(8,128)}), f32[3,2,4,8,192]{4,3,0,2,1:T(8,128)}) %all-reduce.15.cloned.1.call-update) | async-done | bytes 147472
  230.3 10.5 %psum.68 = f32[3,2,1,8,192]{4,3,0,2,1:T(8,128)S(1)} all-reduce(f32[3,2,1,8,192]{4,3,0,2,1:T(8,128)S(1)} %constant_dynamic-slice_fusion.3), channel_id=1, replica_groups=mesh['face'=2,'fy'=4,'fx'=4] {'fy'}, use_global_device_ids=true, to_apply=%region_8.9 | all-reduce | flops 9216 | bytes 73728 | tf_op jit(solution)/shard_map/psum | solution.py:237
  241.7 18.2 %psum.69 = f32[3,2,1,8,192]{4,1,3,2,0:T(2,128)S(1)} all-reduce(f32[3,2,1,8,192]{4,1,3,2,0:T(2,128)S(1)} %copy.314), channel_id=1, replica_groups=mesh['face'=2,'fy'=4,'fx'=4] {'fx'}, use_global_device_ids=true, to_apply=%region_10.11 | all-reduce | flops 9216 | bytes 73728 | tf_op jit(solution)/shard_map/psum | solution.py:238
  264.5 4.5 %collective-permute-start.12 = (f32[3,8,1,192]{3,2,0,1:T(1,128)S(1)}, f32[3,8,1,192]{3,2,0,1:T(1,128)S(1)}, u32[]{:S(2)}, u32[]{:S(2)}) collective-permute-start(f32[3,8,1,192]{3,2,0,1:T(1,128)S(1)} %get-tuple-element.226), channel_id=1, source_target_pairs={{0,1},{1,2},{2,3},{4,5},{5,6},{6,7},{8,9},{9,10},{10,11},{12,13},{... | collective-permute-start | bytes 55304 | tf_op jit(solution)/shard_map/ppermute | solution.py:19
  276.7 3.4 all-to-all-start.6
  280.9 4.0 %all-to-all-done.6 = f32[6,3,8,192]{3,2,1,0:T(8,128)S(1)} async-done(((f32[6,3,8,192]{3,2,1,0:T(8,128)}), f32[6,3,8,192]{3,2,1,0:T(8,128)S(1)}, u32[]{:S(2)}, u32[]{:S(2)}) %all-to-all-start.6) | async-done | bytes 110624 | tf_op jit(solution)/shard_map/all_to_all | solution.py:214
  284.9 3.4 all-to-all-start.7
  288.9 4.2 %all-to-all-done.7 = f32[6,3,8,192]{3,2,1,0:T(8,128)S(1)} async-done(((f32[6,3,8,192]{3,2,1,0:T(8,128)}), f32[6,3,8,192]{3,2,1,0:T(8,128)S(1)}, u32[]{:S(2)}, u32[]{:S(2)}) %all-to-all-start.7) | async-done | bytes 110624 | tf_op jit(solution)/shard_map/all_to_all | solution.py:215
  296.4 34.9 %all-reduce.17.cloned.1.call-done = f32[3,2,4,8,192]{4,3,0,2,1:T(8,128)} async-done(((f32[3,2,4,8,192]{4,3,0,2,1:T(8,128)}), f32[3,2,4,8,192]{4,3,0,2,1:T(8,128)}) %all-reduce.17.cloned.1.call-update) | async-done | bytes 147472
  332.8 10.5 %psum.70 = f32[3,2,1,8,192]{4,3,0,2,1:T(8,128)S(1)} all-reduce(f32[3,2,1,8,192]{4,3,0,2,1:T(8,128)S(1)} %constant_dynamic-slice_fusion.2), channel_id=1, replica_groups=mesh['face'=2,'fy'=4,'fx'=4] {'fy'}, use_global_device_ids=true, to_apply=%region_12.13 | all-reduce | flops 9216 | bytes 73728 | tf_op jit(solution)/shard_map/psum | solution.py:237
  344.2 18.2 %psum.71 = f32[3,2,1,8,192]{4,1,3,2,0:T(2,128)S(1)} all-reduce(f32[3,2,1,8,192]{4,1,3,2,0:T(2,128)S(1)} %copy.330), channel_id=1, replica_groups=mesh['face'=2,'fy'=4,'fx'=4] {'fx'}, use_global_device_ids=true, to_apply=%region_14.15 | all-reduce | flops 9216 | bytes 73728 | tf_op jit(solution)/shard_map/psum | solution.py:238
  (284 shorter events, 68.2 us)
Async XLA Ops:
  7.4 19.6 %copy-start = (s32[6,4]{0,1:T(4,128)S(1)}, s32[6,4]{0,1:T(4,128)}, u32[]{:S(2)}) copy-start(s32[6,4]{0,1:T(4,128)} %param.55) | copy-start | bytes 292
  7.4 1.8 copy-start.1
  13.0 39.6 %collective-permute-start.1 = (f32[3,8,1,192]{3,2,1,0:T(1,128)S(1)}, f32[3,8,1,192]{3,2,1,0:T(1,128)S(1)}, u32[]{:S(2)}, u32[]{:S(2)}) collective-permute-start(f32[3,8,1,192]{3,2,1,0:T(1,128)S(1)} %slice.903), channel_id=1, source_target_pairs={{1,0},{2,1},{3,2},{5,4},{6,5},{7,6},{9,8},{10,9},{11,10},{13,12},{... | collective-permute-start | bytes 55304 | tf_op jit(solution)/shard_map/ppermute | solution.py:21
  14.4 38.2 %collective-permute-start = (f32[3,8,1,192]{3,2,0,1:T(1,128)S(1)}, f32[3,8,1,192]{3,2,0,1:T(1,128)S(1)}, u32[]{:S(2)}, u32[]{:S(2)}) collective-permute-start(f32[3,8,1,192]{3,2,0,1:T(1,128)S(1)} %slice.902), channel_id=1, source_target_pairs={{0,1},{1,2},{2,3},{4,5},{5,6},{6,7},{8,9},{9,10},{10,11},{12,13},{... | collective-permute-start | bytes 55304 | tf_op jit(solution)/shard_map/ppermute | solution.py:19
  20.1 10.9 %collective-permute-start.5 = (f32[3,8,1,1]{2,1,0,3:T(8,128)S(1)}, f32[3,8,1,1]{2,1,0,3:T(8,128)S(1)}, u32[]{:S(2)}, u32[]{:S(2)}) collective-permute-start(f32[3,8,1,1]{2,1,0,3:T(8,128)S(1)} %get-tuple-element.263), channel_id=1, source_target_pairs={{1,0},{2,1},{3,2},{5,4},{6,5},{7,6},{9,8},{10,9},{11,10},{13,12},{... | collective-permute-start | bytes 296 | tf_op jit(solution)/shard_map/ppermute | solution.py:21
  21.4 9.6 %collective-permute-start.4 = (f32[3,8,1,1]{2,1,0,3:T(8,128)S(1)}, f32[3,8,1,1]{2,1,0,3:T(8,128)S(1)}, u32[]{:S(2)}, u32[]{:S(2)}) collective-permute-start(f32[3,8,1,1]{2,1,0,3:T(8,128)S(1)} %get-tuple-element.262), channel_id=1, source_target_pairs={{0,1},{1,2},{2,3},{4,5},{5,6},{6,7},{8,9},{9,10},{10,11},{12,13},{... | collective-permute-start | bytes 296 | tf_op jit(solution)/shard_map/ppermute | solution.py:19
  31.1 4.3 %collective-permute-start.7 = (f32[3,1,8,1]{2,1,0,3:T(1,128)S(1)}, f32[3,1,8,1]{2,1,0,3:T(1,128)S(1)}, u32[]{:S(2)}, u32[]{:S(2)}) collective-permute-start(f32[3,1,8,1]{2,1,0,3:T(1,128)S(1)} %get-tuple-element.261), channel_id=1, source_target_pairs={{4,0},{8,4},{12,8},{5,1},{9,5},{13,9},{6,2},{10,6},{14,10},{7,3},{... | collective-permute-start | bytes 296 | tf_op jit(solution)/shard_map/ppermute | solution.py:21
  32.4 3.8 %collective-permute-start.6 = (f32[3,1,8,1]{2,1,0,3:T(1,128)S(1)}, f32[3,1,8,1]{2,1,0,3:T(1,128)S(1)}, u32[]{:S(2)}, u32[]{:S(2)}) collective-permute-start(f32[3,1,8,1]{2,1,0,3:T(1,128)S(1)} %get-tuple-element.260), channel_id=1, source_target_pairs={{0,4},{4,8},{8,12},{1,5},{5,9},{9,13},{2,6},{6,10},{10,14},{3,7},{... | collective-permute-start | bytes 296 | tf_op jit(solution)/shard_map/ppermute | solution.py:19
  37.2 7.0 %all-to-all-start.2 = ((f32[6,3,8,1]{2,3,1,0:T(1,128)}), f32[6,3,8,1]{2,3,1,0:T(1,128)S(1)}, u32[]{:S(2)}, u32[]{:S(2)}) async-start(f32[6,3,8,1]{2,3,1,0:T(1,128)} %broadcast_multiply_fusion.7), calls=%async_computation.2 | async-start | bytes 18432 | tf_op jit(solution)/shard_map/all_to_all | solution.py:214
  44.3 7.0 %all-to-all-start.3 = ((f32[6,3,8,1]{2,3,1,0:T(1,128)}), f32[6,3,8,1]{2,3,1,0:T(1,128)S(1)}, u32[]{:S(2)}, u32[]{:S(2)}) async-start(f32[6,3,8,1]{2,3,1,0:T(1,128)} %broadcast_multiply_fusion.6), calls=%async_computation.3 | async-start | bytes 18432 | tf_op jit(solution)/shard_map/all_to_all | solution.py:215
  52.8 17.7 %collective-permute-start.3 = (f32[3,1,8,192]{3,2,1,0:T(8,128)S(1)}, f32[3,1,8,192]{3,2,1,0:T(8,128)S(1)}, u32[]{:S(2)}, u32[]{:S(2)}) collective-permute-start(f32[3,1,8,192]{3,2,1,0:T(8,128)S(1)} %slice.905), channel_id=1, source_target_pairs={{4,0},{8,4},{12,8},{5,1},{9,5},{13,9},{6,2},{10,6},{14,10},{7,3},{... | collective-permute-start | bytes 55304 | tf_op jit(solution)/shard_map/ppermute | solution.py:21
  54.1 16.4 %collective-permute-start.2 = (f32[3,1,8,192]{3,2,0,1:T(8,128)S(1)}, f32[3,1,8,192]{3,2,0,1:T(8,128)S(1)}, u32[]{:S(2)}, u32[]{:S(2)}) collective-permute-start(f32[3,1,8,192]{3,2,0,1:T(8,128)S(1)} %slice.904), channel_id=1, source_target_pairs={{0,4},{4,8},{8,12},{1,5},{5,9},{9,13},{2,6},{6,10},{10,14},{3,7},{... | collective-permute-start | bytes 55304 | tf_op jit(solution)/shard_map/ppermute | solution.py:19
  71.4 8.0 %all-to-all-start = ((f32[6,3,8,192]{3,2,1,0:T(8,128)}), f32[6,3,8,192]{3,2,1,0:T(8,128)S(1)}, u32[]{:S(2)}, u32[]{:S(2)}) async-start(f32[6,3,8,192]{3,2,1,0:T(8,128)} %broadcast_multiply_fusion.5), calls=%async_computation | async-start | bytes 294912 | tf_op jit(solution)/shard_map/all_to_all | solution.py:214
  79.4 8.0 %all-to-all-start.1 = ((f32[6,3,8,192]{3,2,1,0:T(8,128)}), f32[6,3,8,192]{3,2,1,0:T(8,128)S(1)}, u32[]{:S(2)}, u32[]{:S(2)}) async-start(f32[6,3,8,192]{3,2,1,0:T(8,128)} %broadcast_multiply_fusion.4), calls=%async_computation.1 | async-start | bytes 294912 | tf_op jit(solution)/shard_map/all_to_all | solution.py:215
  82.8 41.7 %all-reduce.13.cloned.1.call-start = ((), (), s32[]{:S(2)}) async-start(), calls=%async_computation.14 | async-start | bytes 393216
  89.7 36.3 %reduce-scatter.7.cloned.1.call-start = ((), (), s32[]{:S(2)}) async-start(), calls=%async_computation.11 | async-start | bytes 245760 | tf_op jit(solution)/shard_map/reduce_scatter | solution.py:240
  160.6 5.9 %collective-permute-start.9 = (f32[3,8,1,192]{3,2,0,1:T(1,128)S(1)}, f32[3,8,1,192]{3,2,0,1:T(1,128)S(1)}, u32[]{:S(2)}, u32[]{:S(2)}) collective-permute-start(f32[3,8,1,192]{3,2,0,1:T(1,128)S(1)} %get-tuple-element.231), channel_id=1, source_target_pairs={{1,0},{2,1},{3,2},{5,4},{6,5},{7,6},{9,8},{10,9},{11,10},{13,12},{... | collective-permute-start | bytes 55304 | tf_op jit(solution)/shard_map/ppermute | solution.py:21
  161.9 6.1 %collective-permute-start.8 = (f32[3,8,1,192]{3,2,0,1:T(1,128)S(1)}, f32[3,8,1,192]{3,2,0,1:T(1,128)S(1)}, u32[]{:S(2)}, u32[]{:S(2)}) collective-permute-start(f32[3,8,1,192]{3,2,0,1:T(1,128)S(1)} %get-tuple-element.230), channel_id=1, source_target_pairs={{0,1},{1,2},{2,3},{4,5},{5,6},{6,7},{8,9},{9,10},{10,11},{12,13},{... | collective-permute-start | bytes 55304 | tf_op jit(solution)/shard_map/ppermute | solution.py:19
  168.0 4.5 %collective-permute-start.11 = (f32[3,1,8,192]{3,2,0,1:T(8,128)S(1)}, f32[3,1,8,192]{3,2,0,1:T(8,128)S(1)}, u32[]{:S(2)}, u32[]{:S(2)}) collective-permute-start(f32[3,1,8,192]{3,2,0,1:T(8,128)S(1)} %get-tuple-element.229), channel_id=1, source_target_pairs={{4,0},{8,4},{12,8},{5,1},{9,5},{13,9},{6,2},{10,6},{14,10},{7,3},{... | collective-permute-start | bytes 55304 | tf_op jit(solution)/shard_map/ppermute | solution.py:21
  169.3 3.9 %collective-permute-start.10 = (f32[3,1,8,192]{3,2,0,1:T(8,128)S(1)}, f32[3,1,8,192]{3,2,0,1:T(8,128)S(1)}, u32[]{:S(2)}, u32[]{:S(2)}) collective-permute-start(f32[3,1,8,192]{3,2,0,1:T(8,128)S(1)} %get-tuple-element.228), channel_id=1, source_target_pairs={{0,4},{4,8},{8,12},{1,5},{5,9},{9,13},{2,6},{6,10},{10,14},{3,7},{... | collective-permute-start | bytes 55304 | tf_op jit(solution)/shard_map/ppermute | solution.py:19
  174.1 8.2 %all-to-all-start.4 = ((f32[6,3,8,192]{3,2,1,0:T(8,128)}), f32[6,3,8,192]{3,2,1,0:T(8,128)S(1)}, u32[]{:S(2)}, u32[]{:S(2)}) async-start(f32[6,3,8,192]{3,2,1,0:T(8,128)} %broadcast_multiply_fusion.3), calls=%async_computation.4 | async-start | bytes 294912 | tf_op jit(solution)/shard_map/all_to_all | solution.py:214
  182.3 8.2 %all-to-all-start.5 = ((f32[6,3,8,192]{3,2,1,0:T(8,128)}), f32[6,3,8,192]{3,2,1,0:T(8,128)S(1)}, u32[]{:S(2)}, u32[]{:S(2)}) async-start(f32[6,3,8,192]{3,2,1,0:T(8,128)} %broadcast_multiply_fusion.2), calls=%async_computation.5 | async-start | bytes 294912 | tf_op jit(solution)/shard_map/all_to_all | solution.py:215
  185.7 43.1 %all-reduce.15.cloned.1.call-start = ((), (), s32[]{:S(2)}) async-start(), calls=%async_computation.15 | async-start | bytes 393216
  192.8 48.1 %reduce-scatter.9.cloned.1.call-start = ((), (), s32[]{:S(2)}) async-start(), calls=%async_computation.12 | async-start | bytes 245760 | tf_op jit(solution)/shard_map/reduce_scatter | solution.py:240
  263.2 5.9 %collective-permute-start.13 = (f32[3,8,1,192]{3,2,0,1:T(1,128)S(1)}, f32[3,8,1,192]{3,2,0,1:T(1,128)S(1)}, u32[]{:S(2)}, u32[]{:S(2)}) collective-permute-start(f32[3,8,1,192]{3,2,0,1:T(1,128)S(1)} %get-tuple-element.227), channel_id=1, source_target_pairs={{1,0},{2,1},{3,2},{5,4},{6,5},{7,6},{9,8},{10,9},{11,10},{13,12},{... | collective-permute-start | bytes 55304 | tf_op jit(solution)/shard_map/ppermute | solution.py:21
  264.5 6.1 %collective-permute-start.12 = (f32[3,8,1,192]{3,2,0,1:T(1,128)S(1)}, f32[3,8,1,192]{3,2,0,1:T(1,128)S(1)}, u32[]{:S(2)}, u32[]{:S(2)}) collective-permute-start(f32[3,8,1,192]{3,2,0,1:T(1,128)S(1)} %get-tuple-element.226), channel_id=1, source_target_pairs={{0,1},{1,2},{2,3},{4,5},{5,6},{6,7},{8,9},{9,10},{10,11},{12,13},{... | collective-permute-start | bytes 55304 | tf_op jit(solution)/shard_map/ppermute | solution.py:19
  270.6 4.3 %collective-permute-start.15 = (f32[3,1,8,192]{3,2,0,1:T(8,128)S(1)}, f32[3,1,8,192]{3,2,0,1:T(8,128)S(1)}, u32[]{:S(2)}, u32[]{:S(2)}) collective-permute-start(f32[3,1,8,192]{3,2,0,1:T(8,128)S(1)} %get-tuple-element.225), channel_id=1, source_target_pairs={{4,0},{8,4},{12,8},{5,1},{9,5},{13,9},{6,2},{10,6},{14,10},{7,3},{... | collective-permute-start | bytes 55304 | tf_op jit(solution)/shard_map/ppermute | solution.py:21
  271.9 3.9 %collective-permute-start.14 = (f32[3,1,8,192]{3,2,0,1:T(8,128)S(1)}, f32[3,1,8,192]{3,2,0,1:T(8,128)S(1)}, u32[]{:S(2)}, u32[]{:S(2)}) collective-permute-start(f32[3,1,8,192]{3,2,0,1:T(8,128)S(1)} %get-tuple-element.224), channel_id=1, source_target_pairs={{0,4},{4,8},{8,12},{1,5},{5,9},{9,13},{2,6},{6,10},{10,14},{3,7},{... | collective-permute-start | bytes 55304 | tf_op jit(solution)/shard_map/ppermute | solution.py:19
  276.7 8.2 %all-to-all-start.6 = ((f32[6,3,8,192]{3,2,1,0:T(8,128)}), f32[6,3,8,192]{3,2,1,0:T(8,128)S(1)}, u32[]{:S(2)}, u32[]{:S(2)}) async-start(f32[6,3,8,192]{3,2,1,0:T(8,128)} %broadcast_multiply_fusion.1), calls=%async_computation.6 | async-start | bytes 294912 | tf_op jit(solution)/shard_map/all_to_all | solution.py:214
  284.9 8.2 %all-to-all-start.7 = ((f32[6,3,8,192]{3,2,1,0:T(8,128)}), f32[6,3,8,192]{3,2,1,0:T(8,128)S(1)}, u32[]{:S(2)}, u32[]{:S(2)}) async-start(f32[6,3,8,192]{3,2,1,0:T(8,128)} %broadcast_multiply_fusion), calls=%async_computation.7 | async-start | bytes 294912 | tf_op jit(solution)/shard_map/all_to_all | solution.py:215
  288.4 43.0 %all-reduce.17.cloned.1.call-start = ((), (), s32[]{:S(2)}) async-start(), calls=%async_computation.16 | async-start | bytes 393216
  295.4 48.0 %reduce-scatter.11.cloned.1.call-start = ((), (), s32[]{:S(2)}) async-start(), calls=%async_computation.13 | async-start | bytes 245760 | tf_op jit(solution)/shard_map/reduce_scatter | solution.py:240
  (8 other events, 5.8 us)
Sparse Core Ops, SparseCore 0:
  89.8 34.6 all-reduce.12
  192.9 35.8 all-reduce.14
  295.5 35.7 all-reduce.16
Sparse Core Ops, SparseCore 1:
  92.6 19.4 reduce-scatter.6
  195.7 20.6 reduce-scatter.8
  298.3 20.6 reduce-scatter.10
where the time goes:
time: 373 us; the launch traced here: 371 us
  waiting for transfers between devices  139 us (37%)
  blocking collectives  99.7 us (27%)
  starting transfers between devices  69.1 us (19%)
  local copies, waits for them, and re-layouts  26.4 us (7%)
  between operations  16.4 us (4%)
  other arithmetic  12.6 us (3%)
  matrix products  7.16 us (2%)
    unnamed x9, waiting for transfers between devices  103 us
    psum x3, blocking collectives, assemble(): tall_whole = lax.psum(tall_lines, 'fx')  54.8 us
    psum x3, blocking collectives, assemble(): flat_whole = lax.psum(flat_lines, 'fy')  31.7 us
    ppermute x8, starting transfers between devices, padded(): lax.ppermute(tail, axis, [(i, (i + 1) % count) for i in range(ends)])  31.5 us
    all_to_all x4, waiting for transfers between devices, assemble(): lax.all_to_all(send_tall, 'face', split_axis=0, concat_axis=1, tiled=True)  16.2 us
    all_to_all x4, waiting for transfers between devices, assemble(): lax.all_to_all(send_flat, 'face', split_axis=0, concat_axis=1, tiled=True)  14.9 us
    all_to_all x4, starting transfers between devices, assemble(): lax.all_to_all(send_flat, 'face', split_axis=0, concat_axis=1, tiled=True)  13.5 us
    all_to_all x4, starting transfers between devices, assemble(): lax.all_to_all(send_tall, 'face', split_axis=0, concat_axis=1, tiled=True)  13.5 us
  transfers between devices with their start and end apart: 30, of which 16 were waited for; matrix products, arithmetic and copies ran while one was open for 5% of the time, Pallas kernels for 0%

commit v1 on v0

--- a/solution.py
+++ b/solution.py
@@ -235,7 +235,13 @@
     tall_lines = jnp.stack([rim_strips[:, 1], rim_strips[:, 3, ::-1]], axis=1)
     tall_lines = tall_lines.reshape(face_local, 2, lax.axis_size("fy"), row_count, chan_count)
     flat_whole = lax.psum(flat_lines, "fy")
-    tall_whole = lax.psum(tall_lines, "fx")
+    size = lax.axis_size("fx")
+    tall_whole, hop = (tall_lines, 1)
+    while hop < size:
+        tall_whole = tall_whole + lax.ppermute(
+            tall_whole, "fx", [(i_2, i_2 ^ hop) for i_2 in range(size)]
+        )
+        hop = 2 * hop
     flat_block = lax.psum_scatter(flat_whole, "fx", scatter_dimension=2, tiled=True)
     tall_block = lax.psum_scatter(tall_whole, "fy", scatter_dimension=2, tiled=True)
     flat_add = jnp.where(on_south, flat_block[:, 0, 0], flat_block[:, 1, 0])

time: 373 us -> 402 us (1.078)
  waiting for transfers between devices: 139 us -> 202 us
  blocking collectives: 99.7 us -> 49.5 us
  starting transfers between devices: 69.1 us -> 86 us
    reduce_scatter x3, waiting for transfers between devices: 0.05 us -> 59 us  [assemble(): lax.psum_scatter(tall_whole, 'fy', scatter_dimension=2, tiled=True)]
    psum x3 -> x0, blocking collectives: 54.8 us -> none  [assemble(): tall_whole = lax.psum(tall_lines, 'fx')]
    ppermute x0 -> x8, starting transfers between devices: none -> 16.9 us  [assemble(): lax.ppermute(tall_whole, 'fx', [(i_2, i_2 ^ hop) for i_2 in range(size)])]
    ppermute x0 -> x8, waiting for transfers between devices: none -> 11.4 us  [assemble(): lax.ppermute(tall_whole, 'fx', [(i_2, i_2 ^ hop) for i_2 in range(size)])]
    unnamed x9, waiting for transfers between devices: 103 us -> 95.2 us
    unnamed x1, blocking collectives: 13.3 us -> 17.8 us
    unnamed x33 -> x32, local copies, waits for them, and re-layouts: 10.3 us -> 9.88 us
  transfers between devices with their start and end apart: 30 -> 38, of which waited for: 16 -> 23; matrix products, arithmetic and copies ran while one was open for 5% -> 5% of each run, Pallas kernels for 0% -> 0%
where the time goes in v1:
time: 402 us; the launch traced here: 400 us
  waiting for transfers between devices  202 us (50%)
  starting transfers between devices  86 us (21%)
  blocking collectives  49.5 us (12%)
  local copies, waits for them, and re-layouts  23.8 us (6%)
  between operations  16.4 us (4%)
  other arithmetic  15.5 us (4%)
  matrix products  7.15 us (2%)
    unnamed x9, waiting for transfers between devices  95.2 us
    reduce_scatter x3, waiting for transfers between devices, assemble(): lax.psum_scatter(tall_whole, 'fy', scatter_dimension=2, tiled=True)  59 us
    psum x3, blocking collectives, assemble(): flat_whole = lax.psum(flat_lines, 'fy')  31.7 us
    ppermute x8, starting transfers between devices, padded(): lax.ppermute(tail, axis, [(i, (i + 1) % count) for i in range(ends)])  31.5 us
    unnamed x1, blocking collectives  17.8 us
    ppermute x8, starting transfers between devices, assemble(): lax.ppermute(tall_whole, 'fx', [(i_2, i_2 ^ hop) for i_2 in range(size)])  16.9 us
    all_to_all x4, waiting for transfers between devices, assemble(): lax.all_to_all(send_tall, 'face', split_axis=0, concat_axis=1, tiled=True)  15.8 us
    all_to_all x4, waiting for transfers between devices, assemble(): lax.all_to_all(send_flat, 'face', split_axis=0, concat_axis=1, tiled=True)  14.8 us
  transfers between devices with their start and end apart: 38, of which 23 were waited for; matrix products, arithmetic and copies ran while one was open for 5% of the time, Pallas kernels for 0%

profile of v1, /device:TPU:0, one launch (start us, length us, event | category | flops | bytes accessed | tf_op | source)
XLA Modules:
  0.0 399.9 jit_solution(4618866222065723823)
XLA Ops:
  14.4 5.6 %collective-permute-start = (f32[3,8,1,192]{3,2,0,1:T(1,128)S(1)}, f32[3,8,1,192]{3,2,0,1:T(1,128)S(1)}, u32[]{:S(2)}, u32[]{:S(2)}) collective-permute-start(f32[3,8,1,192]{3,2,0,1:T(1,128)S(1)} %slice.902), channel_id=1, source_target_pairs={{0,1},{1,2},{2,3},{4,5},{5,6},{6,7},{8,9},{9,10},{10,11},{12,13},{... | collective-permute-start | bytes 55304 | tf_op jit(solution)/shard_map/ppermute | solution.py:19
  21.4 4.5 %collective-permute-start.6 = (f32[3,8,1,1]{2,1,0,3:T(8,128)S(1)}, f32[3,8,1,1]{2,1,0,3:T(8,128)S(1)}, u32[]{:S(2)}, u32[]{:S(2)}) collective-permute-start(f32[3,8,1,1]{2,1,0,3:T(8,128)S(1)} %get-tuple-element.268), channel_id=1, source_target_pairs={{0,1},{1,2},{2,3},{4,5},{5,6},{6,7},{8,9},{9,10},{10,11},{12,13},{... | collective-permute-start | bytes 296 | tf_op jit(solution)/shard_map/ppermute | solution.py:19
  37.2 3.2 all-to-all-start.2
  44.2 3.2 all-to-all-start.3
  47.6 3.7 all-to-all-done.3
  55.3 17.8 %all-reduce.3 = f32[3,2,4,8,1]{3,1,4,0,2:T(2,128)S(1)} all-reduce(f32[3,2,4,8,1]{3,1,4,0,2:T(2,128)S(1)} %copy.287), channel_id=4, replica_groups=mesh['face'=2,'fy'=4,'fx'=4] {'fx'}, use_global_device_ids=true, to_apply=%region_4.5.clone | all-reduce | flops 192 | bytes 1536
  79.4 3.4 all-to-all-start
  83.7 3.8 all-to-all-done
  87.4 3.4 all-to-all-start.1
  91.3 4.1 %all-to-all-done.1 = f32[6,3,8,192]{3,2,1,0:T(8,128)S(1)} async-done(((f32[6,3,8,192]{3,2,1,0:T(8,128)}), f32[6,3,8,192]{3,2,1,0:T(8,128)S(1)}, u32[]{:S(2)}, u32[]{:S(2)}) %all-to-all-start.1) | async-done | bytes 110624 | tf_op jit(solution)/shard_map/all_to_all | solution.py:215
  98.4 6.1 %collective-permute-done.4 = f32[3,2,4,8,192]{4,3,1,0,2:T(8,128)S(1)} collective-permute-done((f32[3,2,4,8,192]{4,3,1,0,2:T(8,128)S(1)}, f32[3,2,4,8,192]{4,3,1,0,2:T(8,128)S(1)}, u32[]{:S(2)}, u32[]{:S(2)}) %collective-permute-start.4) | collective-permute-done | bytes 147488 | tf_op jit(solution)/shard_map/ppermute | solution.py:241
  107.5 32.3 %all-reduce.12.cloned.1.call-done = f32[3,2,4,8,192]{4,3,0,2,1:T(8,128)} async-done(((f32[3,2,4,8,192]{4,3,0,2,1:T(8,128)}), f32[3,2,4,8,192]{4,3,0,2,1:T(8,128)}) %all-reduce.12.cloned.1.call-update) | async-done | bytes 147472
  141.3 10.7 %all-reduce.7 = (f32[3,2,1,8,192]{4,3,0,2,1:T(8,128)S(1)}, f32[3,2,1,8,1]{3,1,4,0,2:T(2,128)S(1)}, f32[3,2,4,8,1]{3,1,4,0,2:T(2,128)S(1)}) all-reduce(f32[3,2,1,8,192]{4,3,0,2,1:T(8,128)S(1)} %constant_dynamic-slice_fusion.5, f32[3,2,1,8,1]{3,1,4,0,2:T(2,128)S(1)} %constant_dynamic-slice_fusion.4, ...), channel_id=1, replica_groups=mesh['face'=2,'fy'=4,'fx'=4] {'fy'}, use_global_device_ids=true, to_apply=%region_0.1 | all-reduce | flops 9456 | bytes 75648 | tf_op jit(solution)/shard_map/psum | solution.py:237
  154.1 19.5 %reduce-scatter.7.cloned.1.call-done = f32[3,2,1,8,192]{4,3,1,0,2:T(8,128)} async-done(((f32[3,2,4,8,192]{4,3,1,0,2:T(8,128)}), f32[3,2,1,8,192]{4,3,1,0,2:T(8,128)}) %reduce-scatter.7.cloned.1.call-update) | async-done | bytes 36880 | tf_op jit(solution)/shard_map/reduce_scatter | solution.py:246
  179.0 4.5 %collective-permute-start.12 = (f32[3,8,1,192]{3,2,0,1:T(1,128)S(1)}, f32[3,8,1,192]{3,2,0,1:T(1,128)S(1)}, u32[]{:S(2)}, u32[]{:S(2)}) collective-permute-start(f32[3,8,1,192]{3,2,0,1:T(1,128)S(1)} %get-tuple-element.230), channel_id=1, source_target_pairs={{0,1},{1,2},{2,3},{4,5},{5,6},{6,7},{8,9},{9,10},{10,11},{12,13},{... | collective-permute-start | bytes 55304 | tf_op jit(solution)/shard_map/ppermute | solution.py:19
  186.5 3.2 collective-permute-start.14
  191.3 3.4 all-to-all-start.4
  195.5 4.0 all-to-all-done.4
  199.4 3.4 all-to-all-start.5
  203.4 4.1 %all-to-all-done.5 = f32[6,3,8,192]{3,2,1,0:T(8,128)S(1)} async-done(((f32[6,3,8,192]{3,2,1,0:T(8,128)}), f32[6,3,8,192]{3,2,1,0:T(8,128)S(1)}, u32[]{:S(2)}, u32[]{:S(2)}) %all-to-all-start.5) | async-done | bytes 110624 | tf_op jit(solution)/shard_map/all_to_all | solution.py:215
  215.1 3.1 collective-permute-start.17
  218.2 31.4 %all-reduce.14.cloned.1.call-done = f32[3,2,4,8,192]{4,3,0,2,1:T(8,128)} async-done(((f32[3,2,4,8,192]{4,3,0,2,1:T(8,128)}), f32[3,2,4,8,192]{4,3,0,2,1:T(8,128)}) %all-reduce.14.cloned.1.call-update) | async-done | bytes 147472
  251.1 10.5 %psum.34 = f32[3,2,1,8,192]{4,3,0,2,1:T(8,128)S(1)} all-reduce(f32[3,2,1,8,192]{4,3,0,2,1:T(8,128)S(1)} %constant_dynamic-slice_fusion.3), channel_id=1, replica_groups=mesh['face'=2,'fy'=4,'fx'=4] {'fy'}, use_global_device_ids=true, to_apply=%region_6.7 | all-reduce | flops 9216 | bytes 73728 | tf_op jit(solution)/shard_map/psum | solution.py:237
  262.4 19.7 %reduce-scatter.9.cloned.1.call-done = f32[3,2,1,8,192]{4,3,1,0,2:T(8,128)} async-done(((f32[3,2,4,8,192]{4,3,1,0,2:T(8,128)}), f32[3,2,1,8,192]{4,3,1,0,2:T(8,128)}) %reduce-scatter.9.cloned.1.call-update) | async-done | bytes 36880 | tf_op jit(solution)/shard_map/reduce_scatter | solution.py:246
  287.5 4.5 %collective-permute-start.18 = (f32[3,8,1,192]{3,2,0,1:T(1,128)S(1)}, f32[3,8,1,192]{3,2,0,1:T(1,128)S(1)}, u32[]{:S(2)}, u32[]{:S(2)}) collective-permute-start(f32[3,8,1,192]{3,2,0,1:T(1,128)S(1)} %get-tuple-element.226), channel_id=1, source_target_pairs={{0,1},{1,2},{2,3},{4,5},{5,6},{6,7},{8,9},{9,10},{10,11},{12,13},{... | collective-permute-start | bytes 55304 | tf_op jit(solution)/shard_map/ppermute | solution.py:19
  299.7 3.4 all-to-all-start.6
  303.9 4.0 all-to-all-done.6
  307.9 3.4 all-to-all-start.7
  311.8 4.1 %all-to-all-done.7 = f32[6,3,8,192]{3,2,1,0:T(8,128)S(1)} async-done(((f32[6,3,8,192]{3,2,1,0:T(8,128)}), f32[6,3,8,192]{3,2,1,0:T(8,128)S(1)}, u32[]{:S(2)}, u32[]{:S(2)}) %all-to-all-start.7) | async-done | bytes 110624 | tf_op jit(solution)/shard_map/all_to_all | solution.py:215
  326.7 31.4 %all-reduce.16.cloned.1.call-done = f32[3,2,4,8,192]{4,3,0,2,1:T(8,128)} async-done(((f32[3,2,4,8,192]{4,3,0,2,1:T(8,128)}), f32[3,2,4,8,192]{4,3,0,2,1:T(8,128)}) %all-reduce.16.cloned.1.call-update) | async-done | bytes 147472
  359.6 10.5 %psum.35 = f32[3,2,1,8,192]{4,3,0,2,1:T(8,128)S(1)} all-reduce(f32[3,2,1,8,192]{4,3,0,2,1:T(8,128)S(1)} %constant_dynamic-slice_fusion.2), channel_id=1, replica_groups=mesh['face'=2,'fy'=4,'fx'=4] {'fy'}, use_global_device_ids=true, to_apply=%region_9.10 | all-reduce | flops 9216 | bytes 73728 | tf_op jit(solution)/shard_map/psum | solution.py:237
  370.9 19.7 %reduce-scatter.11.cloned.1.call-done = f32[3,2,1,8,192]{4,3,1,0,2:T(8,128)} async-done(((f32[3,2,4,8,192]{4,3,1,0,2:T(8,128)}), f32[3,2,1,8,192]{4,3,1,0,2:T(8,128)}) %reduce-scatter.11.cloned.1.call-update) | async-done | bytes 36880 | tf_op jit(solution)/shard_map/reduce_scatter | solution.py:246
  (305 shorter events, 93.7 us)
Async XLA Ops:
  13.0 60.1 %collective-permute-start.1 = (f32[3,8,1,192]{3,2,1,0:T(1,128)S(1)}, f32[3,8,1,192]{3,2,1,0:T(1,128)S(1)}, u32[]{:S(2)}, u32[]{:S(2)}) collective-permute-start(f32[3,8,1,192]{3,2,1,0:T(1,128)S(1)} %slice.903), channel_id=1, source_target_pairs={{1,0},{2,1},{3,2},{5,4},{6,5},{7,6},{9,8},{10,9},{11,10},{13,12},{... | collective-permute-start | bytes 55304 | tf_op jit(solution)/shard_map/ppermute | solution.py:21
  14.4 58.8 %collective-permute-start = (f32[3,8,1,192]{3,2,0,1:T(1,128)S(1)}, f32[3,8,1,192]{3,2,0,1:T(1,128)S(1)}, u32[]{:S(2)}, u32[]{:S(2)}) collective-permute-start(f32[3,8,1,192]{3,2,0,1:T(1,128)S(1)} %slice.902), channel_id=1, source_target_pairs={{0,1},{1,2},{2,3},{4,5},{5,6},{6,7},{8,9},{9,10},{10,11},{12,13},{... | collective-permute-start | bytes 55304 | tf_op jit(solution)/shard_map/ppermute | solution.py:19
  20.1 10.9 %collective-permute-start.7 = (f32[3,8,1,1]{2,1,0,3:T(8,128)S(1)}, f32[3,8,1,1]{2,1,0,3:T(8,128)S(1)}, u32[]{:S(2)}, u32[]{:S(2)}) collective-permute-start(f32[3,8,1,1]{2,1,0,3:T(8,128)S(1)} %get-tuple-element.269), channel_id=1, source_target_pairs={{1,0},{2,1},{3,2},{5,4},{6,5},{7,6},{9,8},{10,9},{11,10},{13,12},{... | collective-permute-start | bytes 296 | tf_op jit(solution)/shard_map/ppermute | solution.py:21
  21.4 9.6 %collective-permute-start.6 = (f32[3,8,1,1]{2,1,0,3:T(8,128)S(1)}, f32[3,8,1,1]{2,1,0,3:T(8,128)S(1)}, u32[]{:S(2)}, u32[]{:S(2)}) collective-permute-start(f32[3,8,1,1]{2,1,0,3:T(8,128)S(1)} %get-tuple-element.268), channel_id=1, source_target_pairs={{0,1},{1,2},{2,3},{4,5},{5,6},{6,7},{8,9},{9,10},{10,11},{12,13},{... | collective-permute-start | bytes 296 | tf_op jit(solution)/shard_map/ppermute | solution.py:19
  37.2 7.0 %all-to-all-start.2 = ((f32[6,3,8,1]{2,3,1,0:T(1,128)}), f32[6,3,8,1]{2,3,1,0:T(1,128)S(1)}, u32[]{:S(2)}, u32[]{:S(2)}) async-start(f32[6,3,8,1]{2,3,1,0:T(1,128)} %broadcast_multiply_fusion.7), calls=%async_computation.3 | async-start | bytes 18432 | tf_op jit(solution)/shard_map/all_to_all | solution.py:214
  44.2 7.0 %all-to-all-start.3 = ((f32[6,3,8,1]{2,3,1,0:T(1,128)}), f32[6,3,8,1]{2,3,1,0:T(1,128)S(1)}, u32[]{:S(2)}, u32[]{:S(2)}) async-start(f32[6,3,8,1]{2,3,1,0:T(1,128)} %broadcast_multiply_fusion.6), calls=%async_computation.4 | async-start | bytes 18432 | tf_op jit(solution)/shard_map/all_to_all | solution.py:215
  52.8 20.3 %collective-permute-start.10 = (f32[3,2,4,8,1]{3,1,4,0,2:T(2,128)S(1)}, f32[3,2,4,8,1]{3,1,4,0,2:T(2,128)S(1)}, u32[]{:S(2)}, u32[]{:S(2)}) collective-permute-start(f32[3,2,4,8,1]{3,1,4,0,2:T(2,128)S(1)} %copy.291), channel_id=1, source_target_pairs={{0,1},{1,0},{2,3},{3,2},{4,5},{5,4},{6,7},{7,6},{8,9},{9,8},{10,11... | collective-permute-start | bytes 2312 | tf_op jit(solution)/shard_map/ppermute | solution.py:241
  73.1 5.3 %collective-permute-start.11 = (f32[3,2,4,8,1]{3,1,4,0,2:T(2,128)S(1)}, f32[3,2,4,8,1]{3,1,4,0,2:T(2,128)S(1)}, u32[]{:S(2)}, u32[]{:S(2)}) collective-permute-start(f32[3,2,4,8,1]{3,1,4,0,2:T(2,128)S(1)} %copy_add_fusion), channel_id=1, source_target_pairs={{0,2},{1,3},{2,0},{3,1},{4,6},{5,7},{6,4},{7,5},{8,10},{9,11},{10,... | collective-permute-start | bytes 2312 | tf_op jit(solution)/shard_map/ppermute | solution.py:241
  73.3 5.1 %collective-permute-start.3 = (f32[3,1,8,192]{3,2,1,0:T(8,128)S(1)}, f32[3,1,8,192]{3,2,1,0:T(8,128)S(1)}, u32[]{:S(2)}, u32[]{:S(2)}) collective-permute-start(f32[3,1,8,192]{3,2,1,0:T(8,128)S(1)} %slice.905), channel_id=1, source_target_pairs={{4,0},{8,4},{12,8},{5,1},{9,5},{13,9},{6,2},{10,6},{14,10},{7,3},{... | collective-permute-start | bytes 55304 | tf_op jit(solution)/shard_map/ppermute | solution.py:21
  79.4 8.0 %all-to-all-start = ((f32[6,3,8,192]{3,2,1,0:T(8,128)}), f32[6,3,8,192]{3,2,1,0:T(8,128)S(1)}, u32[]{:S(2)}, u32[]{:S(2)}) async-start(f32[6,3,8,192]{3,2,1,0:T(8,128)} %broadcast_multiply_fusion.5), calls=%async_computation | async-start | bytes 294912 | tf_op jit(solution)/shard_map/all_to_all | solution.py:214
  87.4 8.0 %all-to-all-start.1 = ((f32[6,3,8,192]{3,2,1,0:T(8,128)}), f32[6,3,8,192]{3,2,1,0:T(8,128)S(1)}, u32[]{:S(2)}, u32[]{:S(2)}) async-start(f32[6,3,8,192]{3,2,1,0:T(8,128)} %broadcast_multiply_fusion.4), calls=%async_computation.1 | async-start | bytes 294912 | tf_op jit(solution)/shard_map/all_to_all | solution.py:215
  90.8 49.0 %all-reduce.12.cloned.1.call-start = ((), (), s32[]{:S(2)}) async-start(), calls=%async_computation.14 | async-start | bytes 393216
  97.0 7.5 %collective-permute-start.4 = (f32[3,2,4,8,192]{4,3,1,0,2:T(8,128)S(1)}, f32[3,2,4,8,192]{4,3,1,0,2:T(8,128)S(1)}, u32[]{:S(2)}, u32[]{:S(2)}) collective-permute-start(f32[3,2,4,8,192]{4,3,1,0,2:T(8,128)S(1)} %copy.281), channel_id=1, source_target_pairs={{0,1},{1,0},{2,3},{3,2},{4,5},{5,4},{6,7},{7,6},{8,9},{9,8},{10,11... | collective-permute-start | bytes 442376 | tf_op jit(solution)/shard_map/ppermute | solution.py:241
  98.3 75.4 %reduce-scatter.7.cloned.1.call-start = ((), (), s32[]{:S(2)}) async-start(), calls=%async_computation.11 | async-start | bytes 245760 | tf_op jit(solution)/shard_map/reduce_scatter | solution.py:246
  104.5 48.6 %collective-permute-start.5 = (f32[3,2,4,8,192]{4,3,1,0,2:T(8,128)S(1)}, f32[3,2,4,8,192]{4,3,1,0,2:T(8,128)S(1)}, u32[]{:S(2)}, u32[]{:S(2)}) collective-permute-start(f32[3,2,4,8,192]{4,3,1,0,2:T(8,128)S(1)} %copy_add_fusion.3), channel_id=1, source_target_pairs={{0,2},{1,3},{2,0},{3,1},{4,6},{5,7},{6,4},{7,5},{8,10},{9,11},{10,... | collective-permute-start | bytes 442376 | tf_op jit(solution)/shard_map/ppermute | solution.py:241
  177.7 5.9 %collective-permute-start.13 = (f32[3,8,1,192]{3,2,0,1:T(1,128)S(1)}, f32[3,8,1,192]{3,2,0,1:T(1,128)S(1)}, u32[]{:S(2)}, u32[]{:S(2)}) collective-permute-start(f32[3,8,1,192]{3,2,0,1:T(1,128)S(1)} %get-tuple-element.231), channel_id=1, source_target_pairs={{1,0},{2,1},{3,2},{5,4},{6,5},{7,6},{9,8},{10,9},{11,10},{13,12},{... | collective-permute-start | bytes 55304 | tf_op jit(solution)/shard_map/ppermute | solution.py:21
  179.0 6.1 %collective-permute-start.12 = (f32[3,8,1,192]{3,2,0,1:T(1,128)S(1)}, f32[3,8,1,192]{3,2,0,1:T(1,128)S(1)}, u32[]{:S(2)}, u32[]{:S(2)}) collective-permute-start(f32[3,8,1,192]{3,2,0,1:T(1,128)S(1)} %get-tuple-element.230), channel_id=1, source_target_pairs={{0,1},{1,2},{2,3},{4,5},{5,6},{6,7},{8,9},{9,10},{10,11},{12,13},{... | collective-permute-start | bytes 55304 | tf_op jit(solution)/shard_map/ppermute | solution.py:19
  185.2 4.5 %collective-permute-start.15 = (f32[3,1,8,192]{3,2,0,1:T(8,128)S(1)}, f32[3,1,8,192]{3,2,0,1:T(8,128)S(1)}, u32[]{:S(2)}, u32[]{:S(2)}) collective-permute-start(f32[3,1,8,192]{3,2,0,1:T(8,128)S(1)} %get-tuple-element.229), channel_id=1, source_target_pairs={{4,0},{8,4},{12,8},{5,1},{9,5},{13,9},{6,2},{10,6},{14,10},{7,3},{... | collective-permute-start | bytes 55304 | tf_op jit(solution)/shard_map/ppermute | solution.py:21
  191.3 8.1 %all-to-all-start.4 = ((f32[6,3,8,192]{3,2,1,0:T(8,128)}), f32[6,3,8,192]{3,2,1,0:T(8,128)S(1)}, u32[]{:S(2)}, u32[]{:S(2)}) async-start(f32[6,3,8,192]{3,2,1,0:T(8,128)} %broadcast_multiply_fusion.3), calls=%async_computation.5 | async-start | bytes 294912 | tf_op jit(solution)/shard_map/all_to_all | solution.py:214
  199.4 8.0 %all-to-all-start.5 = ((f32[6,3,8,192]{3,2,1,0:T(8,128)}), f32[6,3,8,192]{3,2,1,0:T(8,128)S(1)}, u32[]{:S(2)}, u32[]{:S(2)}) async-start(f32[6,3,8,192]{3,2,1,0:T(8,128)} %broadcast_multiply_fusion.2), calls=%async_computation.6 | async-start | bytes 294912 | tf_op jit(solution)/shard_map/all_to_all | solution.py:215
  202.9 46.7 %all-reduce.14.cloned.1.call-start = ((), (), s32[]{:S(2)}) async-start(), calls=%async_computation.15 | async-start | bytes 393216
  209.0 6.0 %collective-permute-start.16 = (f32[3,2,4,8,192]{4,3,1,0,2:T(8,128)S(1)}, f32[3,2,4,8,192]{4,3,1,0,2:T(8,128)S(1)}, u32[]{:S(2)}, u32[]{:S(2)}) collective-permute-start(f32[3,2,4,8,192]{4,3,1,0,2:T(8,128)S(1)} %copy.321), channel_id=1, source_target_pairs={{0,1},{1,0},{2,3},{3,2},{4,5},{5,4},{6,7},{7,6},{8,9},{9,8},{10,11... | collective-permute-start | bytes 442376 | tf_op jit(solution)/shard_map/ppermute | solution.py:241
  212.4 69.8 %reduce-scatter.9.cloned.1.call-start = ((), (), s32[]{:S(2)}) async-start(), calls=%async_computation.12 | async-start | bytes 245760 | tf_op jit(solution)/shard_map/reduce_scatter | solution.py:246
  215.1 46.5 %collective-permute-start.17 = (f32[3,2,4,8,192]{4,3,1,0,2:T(8,128)S(1)}, f32[3,2,4,8,192]{4,3,1,0,2:T(8,128)S(1)}, u32[]{:S(2)}, u32[]{:S(2)}) collective-permute-start(f32[3,2,4,8,192]{4,3,1,0,2:T(8,128)S(1)} %copy_add_fusion.2), channel_id=1, source_target_pairs={{0,2},{1,3},{2,0},{3,1},{4,6},{5,7},{6,4},{7,5},{8,10},{9,11},{10,... | collective-permute-start | bytes 442376 | tf_op jit(solution)/shard_map/ppermute | solution.py:241
  286.2 5.9 %collective-permute-start.19 = (f32[3,8,1,192]{3,2,0,1:T(1,128)S(1)}, f32[3,8,1,192]{3,2,0,1:T(1,128)S(1)}, u32[]{:S(2)}, u32[]{:S(2)}) collective-permute-start(f32[3,8,1,192]{3,2,0,1:T(1,128)S(1)} %get-tuple-element.227), channel_id=1, source_target_pairs={{1,0},{2,1},{3,2},{5,4},{6,5},{7,6},{9,8},{10,9},{11,10},{13,12},{... | collective-permute-start | bytes 55304 | tf_op jit(solution)/shard_map/ppermute | solution.py:21
  287.5 6.1 %collective-permute-start.18 = (f32[3,8,1,192]{3,2,0,1:T(1,128)S(1)}, f32[3,8,1,192]{3,2,0,1:T(1,128)S(1)}, u32[]{:S(2)}, u32[]{:S(2)}) collective-permute-start(f32[3,8,1,192]{3,2,0,1:T(1,128)S(1)} %get-tuple-element.226), channel_id=1, source_target_pairs={{0,1},{1,2},{2,3},{4,5},{5,6},{6,7},{8,9},{9,10},{10,11},{12,13},{... | collective-permute-start | bytes 55304 | tf_op jit(solution)/shard_map/ppermute | solution.py:19
  299.7 8.1 %all-to-all-start.6 = ((f32[6,3,8,192]{3,2,1,0:T(8,128)}), f32[6,3,8,192]{3,2,1,0:T(8,128)S(1)}, u32[]{:S(2)}, u32[]{:S(2)}) async-start(f32[6,3,8,192]{3,2,1,0:T(8,128)} %broadcast_multiply_fusion.1), calls=%async_computation.8 | async-start | bytes 294912 | tf_op jit(solution)/shard_map/all_to_all | solution.py:214
  307.9 8.0 %all-to-all-start.7 = ((f32[6,3,8,192]{3,2,1,0:T(8,128)}), f32[6,3,8,192]{3,2,1,0:T(8,128)S(1)}, u32[]{:S(2)}, u32[]{:S(2)}) async-start(f32[6,3,8,192]{3,2,1,0:T(8,128)} %broadcast_multiply_fusion), calls=%async_computation.9 | async-start | bytes 294912 | tf_op jit(solution)/shard_map/all_to_all | solution.py:215
  311.3 46.7 %all-reduce.16.cloned.1.call-start = ((), (), s32[]{:S(2)}) async-start(), calls=%async_computation.16 | async-start | bytes 393216
  317.5 6.0 %collective-permute-start.22 = (f32[3,2,4,8,192]{4,3,1,0,2:T(8,128)S(1)}, f32[3,2,4,8,192]{4,3,1,0,2:T(8,128)S(1)}, u32[]{:S(2)}, u32[]{:S(2)}) collective-permute-start(f32[3,2,4,8,192]{4,3,1,0,2:T(8,128)S(1)} %copy.339), channel_id=1, source_target_pairs={{0,1},{1,0},{2,3},{3,2},{4,5},{5,4},{6,7},{7,6},{8,9},{9,8},{10,11... | collective-permute-start | bytes 442376 | tf_op jit(solution)/shard_map/ppermute | solution.py:241
  320.8 69.8 %reduce-scatter.11.cloned.1.call-start = ((), (), s32[]{:S(2)}) async-start(), calls=%async_computation.13 | async-start | bytes 245760 | tf_op jit(solution)/shard_map/reduce_scatter | solution.py:246
  323.5 46.5 %collective-permute-start.23 = (f32[3,2,4,8,192]{4,3,1,0,2:T(8,128)S(1)}, f32[3,2,4,8,192]{4,3,1,0,2:T(8,128)S(1)}, u32[]{:S(2)}, u32[]{:S(2)}) collective-permute-start(f32[3,2,4,8,192]{4,3,1,0,2:T(8,128)S(1)} %copy_add_fusion.1), channel_id=1, source_target_pairs={{0,2},{1,3},{2,0},{3,1},{4,6},{5,7},{6,4},{7,5},{8,10},{9,11},{10,... | collective-permute-start | bytes 442376 | tf_op jit(solution)/shard_map/ppermute | solution.py:241
  (16 other events, 51.4 us)
Sparse Core Ops, SparseCore 0:
  98.4 41.3 all-reduce.11
  212.5 37.0 all-reduce.13
  320.9 37.0 all-reduce.15
Sparse Core Ops, SparseCore 1:
  153.9 19.7 reduce-scatter.6
  262.4 19.7 reduce-scatter.8
  370.9 19.7 reduce-scatter.10
